TPU v7x, 32 devices: a whole 2x2x4 slice. The times are simulated.
32 devices in a mesh: ta: 8 (over y, x, core), ga: 4 (over z).
Axes of the slice: x: 2, y: 2, z: 4, core: 2. Of those that a mesh axis runs over, the one named last changes fastest.
Arguments:
- snapshots: bfloat16 [1024, 4, 16384], P('ta', 'ga'), may hold values from -12 to 12
- block_starts: int32 [7], replicated, may hold values from 0 to 768
- kept_freqs: int32 [32], replicated, may hold values from 0 to 128
Outputs:
- spectra: bfloat16 [4, 7, 2, 32, 16384], P('ga', None, None, None, 'ta')
- power_step: float32 [4, 7, 2, 32, 16384], P('ga', None, None, None, 'ta')
All inputs are finite; a program needn't handle non-finite values.
Results may differ from a plain program's by a relative error of at most 0.0047.
Values may be sent and summed in bfloat16 or wider, within the bound.
A program may use at most 192 MiB of HBM per device.

v0:
```python
import math
import jax
import jax.numpy as jnp
from jax import lax
from jax.sharding import PartitionSpec as P

NFFT = 256
NB = 7
NF = 32


def kernel_table(kept_freqs, sample_index):
    phase_index = kept_freqs[:, None] * sample_index[None, :] % NFFT
    angle_val = 2.0 * math.pi / NFFT * phase_index.astype(jnp.float32)
    window = 0.5 - 0.5 * jnp.cos(2.0 * math.pi / NFFT * sample_index.astype(jnp.float32))
    norm_scale = 2.0 / math.sqrt(NFFT)
    real_rows = window[None, :] * jnp.cos(angle_val) * norm_scale
    imag_rows = -window[None, :] * jnp.sin(angle_val) * norm_scale
    return jnp.concatenate([real_rows, imag_rows], axis=0)


def transform(series, kernel_rows, block_starts):
    blocks = []
    for block_index in range(NB):
        segment = lax.dynamic_slice_in_dim(series, block_starts[block_index], NFFT, 0)
        blocks.append(jnp.dot(kernel_rows, segment, preferred_element_type=jnp.float32))
    return jnp.stack(blocks).astype(jnp.bfloat16)


def gram_terms(spectra):
    values = spectra.reshape(NB, 2, NF, -1)
    real_part = values[:, 0]
    imag_part = values[:, 1]
    f32 = jnp.float32
    gram_re = jnp.einsum(
        "bfp,cfp->fbc", real_part, real_part, preferred_element_type=f32
    ) + jnp.einsum("bfp,cfp->fbc", imag_part, imag_part, preferred_element_type=f32)
    gram_im = jnp.einsum(
        "bfp,cfp->fbc", real_part, imag_part, preferred_element_type=f32
    ) - jnp.einsum("bfp,cfp->fbc", imag_part, real_part, preferred_element_type=f32)
    return (gram_re, gram_im)


def power_apply(spectra, gram_re, gram_im):
    values = spectra.astype(jnp.float32).reshape(NB, 2, NF, -1)
    real_part = values[:, 0]
    imag_part = values[:, 1]
    highest = lax.Precision.HIGHEST
    out_re = jnp.einsum("cfp,fcb->bfp", real_part, gram_re, precision=highest) - jnp.einsum(
        "cfp,fcb->bfp", imag_part, gram_im, precision=highest
    )
    out_im = jnp.einsum("cfp,fcb->bfp", real_part, gram_im, precision=highest) + jnp.einsum(
        "cfp,fcb->bfp", imag_part, gram_re, precision=highest
    )
    return jnp.stack([out_re, out_im], axis=1)


def shards(snapshots, block_starts, kept_freqs):
    ta_count = lax.axis_size("ta")
    ga_count = lax.axis_size("ga")
    local_times = snapshots.shape[0]
    own_pts = snapshots.shape[2] // ta_count
    kernel_rows = kernel_table(kept_freqs, jnp.arange(NFFT, dtype=jnp.int32)).astype(jnp.bfloat16)
    shaped = snapshots.reshape(local_times, ta_count, own_pts)
    arrived = lax.all_to_all(shaped, "ta", split_axis=1, concat_axis=0, tiled=True)
    spectra = transform(
        arrived.reshape(arrived.shape[0], arrived.shape[2]), kernel_rows, block_starts
    )
    late_sums = gram_terms(spectra)
    summed = lax.psum((late_sums[0], late_sums[1]), ("ta", "ga"))
    denominator = float(NB * own_pts * ta_count * ga_count)
    gram_re = summed[0] / denominator
    gram_im = summed[1] / denominator
    power = power_apply(spectra, gram_re, gram_im)
    return (spectra.reshape(1, NB, 2, NF, own_pts), power.reshape(1, NB, 2, NF, own_pts))


def solution(mesh):
    in_specs = (P("ta", "ga", None), P(), P())
    out_specs = (P("ga", None, None, None, "ta"), P("ga", None, None, None, "ta"))
    return jax.shard_map(shards, mesh=mesh, in_specs=in_specs, out_specs=out_specs, check_vma=False)
```

profile of v0, /device:TPU:0, one launch (start us, length us, event | category | flops | bytes accessed | tf_op | source)
XLA Modules:
  0.0 161.5 jit_solution(14835817679543147446)
XLA Ops:
  0.6 6.4 %copy.43 = bf16[128,1,16384]{0,2,1:T(8,128)(2,1)} copy(bf16[128,1,16384]{2,0,1:T(8,128)(2,1)} %param.3) | data formatting | bytes 8388608 | tf_op args[0]
  7.1 5.3 %all-to-all-start = ((bf16[128,8,2048]{0,2,1:T(8,128)(2,1)}), bf16[128,8,2048]{0,2,1:T(8,128)(2,1)}, u32[]{:S(2)}, u32[]{:S(2)}) async-start(bf16[128,8,2048]{0,2,1:T(8,128)(2,1)} %bitcast.61), calls=%async_computation | async-start | bytes 8388608 | tf_op jit(solution)/shard_map/all_to_all | solution.py:65
  12.4 0.0 copy-done.6
  12.4 0.7 fusion.29
  26.2 0.0 copy-done.7
  26.2 0.2 multiply_convert_fusion.1
  26.4 35.2 %all-to-all-done = bf16[128,8,2048]{0,2,1:T(8,128)(2,1)} async-done(((bf16[128,8,2048]{0,2,1:T(8,128)(2,1)}), bf16[128,8,2048]{0,2,1:T(8,128)(2,1)}, u32[]{:S(2)}, u32[]{:S(2)}) %all-to-all-start) | async-done | bytes 4194336 | tf_op jit(solution)/shard_map/all_to_all | solution.py:65
  61.6 6.5 %copy.44 = bf16[8,128,1,2048]{3,1,0,2:T(8,128)(2,1)} copy(bf16[8,128,1,2048]{1,3,0,2:T(8,128)(2,1)} %bitcast.2) | data formatting | bytes 8388608 | tf_op jit(solution)/shard_map/all_to_all | solution.py:65
  68.1 1.8 %convolution_convert_fusion = bf16[64,2048]{1,0:T(8,128)(2,1)S(1)} fusion(bf16[1024,2048]{1,0:T(8,128)(2,1)} %bitcast.54, s32[]{:T(128)S(6)} %select_n.35, bf16[32,256]{1,0:T(8,128)(2,1)S(1)} %get-tuple-element.20, bf16[32,256]{1,0:T(8,128)(2,1)S(1)} %get-tuple-element.19), kind=kOutput, calls=%fused_computation.5 | convolution fusion | flops 67305472 | bytes 1343492 | tf_op jit(solution)/shard_map/dot_general | solution.py:26
  69.9 1.7 %convolution_convert_fusion.1 = bf16[64,2048]{1,0:T(8,128)(2,1)S(1)} fusion(bf16[1024,2048]{1,0:T(8,128)(2,1)} %bitcast.55, s32[]{:T(128)S(6)} %select_n.34, bf16[32,256]{1,0:T(8,128)(2,1)S(1)} %get-tuple-element.20, bf16[32,256]{1,0:T(8,128)(2,1)S(1)} %get-tuple-element.19), kind=kOutput, calls=%fused_computation.6 | convolution fusion | flops 67305472 | bytes 1343492 | tf_op jit(solution)/shard_map/dot_general | solution.py:26
  71.6 1.7 %convolution_convert_fusion.2 = bf16[64,2048]{1,0:T(8,128)(2,1)S(1)} fusion(bf16[1024,2048]{1,0:T(8,128)(2,1)} %bitcast.56, s32[]{:T(128)S(6)} %select_n.33, bf16[32,256]{1,0:T(8,128)(2,1)S(1)} %get-tuple-element.20, bf16[32,256]{1,0:T(8,128)(2,1)S(1)} %get-tuple-element.19), kind=kOutput, calls=%fused_computation.7 | convolution fusion | flops 67305472 | bytes 1343492 | tf_op jit(solution)/shard_map/dot_general | solution.py:26
  73.2 1.7 %convolution_convert_fusion.3 = bf16[64,2048]{1,0:T(8,128)(2,1)S(1)} fusion(bf16[1024,2048]{1,0:T(8,128)(2,1)} %bitcast.57, s32[]{:T(128)S(6)} %select_n.32, bf16[32,256]{1,0:T(8,128)(2,1)S(1)} %get-tuple-element.20, bf16[32,256]{1,0:T(8,128)(2,1)S(1)} %get-tuple-element.19), kind=kOutput, calls=%fused_computation.8 | convolution fusion | flops 67305472 | bytes 1343492 | tf_op jit(solution)/shard_map/dot_general | solution.py:26
  74.9 0.0 copy-done
  74.9 0.4 convolution_convert_fusion.4
  75.3 0.4 convolution_convert_fusion.5
  75.7 0.4 convolution_convert_fusion.6
  76.2 1.2 copy.46
  77.4 1.2 copy.45
  78.6 1.2 copy.47
  79.8 1.2 copy.48
  81.0 1.2 copy.49
  82.2 1.2 copy.50
  83.4 1.2 copy.51
  84.6 9.9 %stack.64 = bf16[7,2,32,2048]{3,0,2,1:T(8,128)(2,1)S(1)} concatenate(bf16[1,2,32,2048]{3,0,2,1:T(2,128)(2,1)} %copy.45, bf16[1,2,32,2048]{3,0,2,1:T(2,128)(2,1)} %copy.46, bf16[1,2,32,2048]{3,0,2,1:T(2,128)(2,1)} %copy.47, bf16[1,2,32,2048]{3,0,2,1:T(2,128)(2,1)} %copy.48, bf16[1,2,32,2048]{3,0,2,1:T(2,128)(2,1)} %copy.49, bf16[1,2,32,2048]{3,0,2,1:T(2,128)(2,1)} %copy.50, ...), dimensions={0} | concatenate | bytes 3670016 | tf_op jit(solution)/shard_map/stack | solution.py:27
  94.5 1.4 fusion.11
  96.0 1.4 fusion.10
  97.4 1.4 fusion.14
  98.8 0.8 fusion.13
  99.5 1.6 %copy.55 = f32[32,7,7]{0,2,1:T(8,128)} copy(f32[32,7,7]{2,1,0:T(8,128)} %fusion.11) | data formatting | bytes 12544 | tf_op jit(solution)/shard_map/bfp,cfp->fbc/dot_general | solution.py:38
  101.2 1.6 %copy.56 = f32[32,7,7]{0,2,1:T(8,128)} copy(f32[32,7,7]{2,1,0:T(8,128)} %fusion.10) | data formatting | bytes 12544 | tf_op jit(solution)/shard_map/bfp,cfp->fbc/dot_general | solution.py:40
  102.8 1.6 %copy.53 = f32[32,7,7]{0,2,1:T(8,128)} copy(f32[32,7,7]{2,1,0:T(8,128)} %fusion.14) | data formatting | bytes 12544 | tf_op jit(solution)/shard_map/bfp,cfp->fbc/dot_general | solution.py:37
  104.4 0.7 copy.52
  105.1 0.8 sub.22
  105.9 0.8 add.48
  106.7 41.2 %all-reduce = (f32[32,7,7]{0,2,1:T(8,128)S(1)}, f32[32,7,7]{0,2,1:T(8,128)S(1)}) all-reduce(f32[32,7,7]{0,2,1:T(8,128)S(1)} %sub.22, f32[32,7,7]{0,2,1:T(8,128)S(1)} %add.48), channel_id=1, replica_groups=mesh['ta'=8,'ga'=4] {'ta','ga'}, use_global_device_ids=true, to_apply=%region_1.2 | all-reduce | flops 3136 | bytes 25088 | tf_op jit(solution)/shard_map/psum | solution.py:70
  147.9 0.6 broadcast_multiply_fusion
  148.5 0.8 copy.54
  149.3 0.9 copy.57
  150.1 0.0 copy-start.4
  150.2 1.0 constant_dynamic-update-slice_fusion.6
  151.2 1.0 fusion.9
  152.2 1.0 fusion.12
  153.1 1.1 fusion
  154.3 1.1 fusion.1
  155.4 0.7 maximum_bitcast_fusion
  156.2 4.0 %copy.60 = f32[1,7,2,32,2048]{4,3,2,1,0:T(8,128)} copy(f32[1,7,2,32,2048]{4,1,3,2,0:T(8,128)S(1)} %maximum_bitcast_fusion) | data formatting | bytes 7340032
  160.3 0.0 copy-start.5
  160.3 1.2 copy-done.5
  (18 shorter events, 0.2 us)
Async XLA Ops:
  7.1 5.3 %copy-start.6 = (s32[7]{0:T(128)S(1)}, s32[7]{0:T(128)}, u32[]{:S(2)}) copy-start(s32[7]{0:T(128)} %param.4) | copy-start | bytes 88
  7.1 19.1 %copy-start.7 = (s32[32]{0:T(128)S(1)}, s32[32]{0:T(128)}, u32[]{:S(2)}) copy-start(s32[32]{0:T(128)} %param.5) | copy-start | bytes 388
  7.1 54.5 %all-to-all-start = ((bf16[128,8,2048]{0,2,1:T(8,128)(2,1)}), bf16[128,8,2048]{0,2,1:T(8,128)(2,1)}, u32[]{:S(2)}, u32[]{:S(2)}) async-start(bf16[128,8,2048]{0,2,1:T(8,128)(2,1)} %bitcast.61), calls=%async_computation | async-start | bytes 8388608 | tf_op jit(solution)/shard_map/all_to_all | solution.py:65
  68.1 6.8 %copy-start = (bf16[8,128,1,2048]{3,1,0,2:T(8,128)(2,1)S(1)}, bf16[8,128,1,2048]{3,1,0,2:T(8,128)(2,1)}, u32[]{:S(2)}) copy-start(bf16[8,128,1,2048]{3,1,0,2:T(8,128)(2,1)} %copy.44) | copy-start | bytes 12582916
  75.7 5.2 %copy-start.1 = (bf16[64,2048]{1,0:T(8,128)(2,1)}, bf16[64,2048]{1,0:T(8,128)(2,1)S(1)}, u32[]{:S(2)}) copy-start(bf16[64,2048]{1,0:T(8,128)(2,1)S(1)} %convolution_convert_fusion.5) | copy-start | bytes 786436
  76.2 7.2 %copy-start.3 = (bf16[64,2048]{1,0:T(8,128)(2,1)}, bf16[64,2048]{1,0:T(8,128)(2,1)S(1)}, u32[]{:S(2)}) copy-start(bf16[64,2048]{1,0:T(8,128)(2,1)S(1)} %convolution_convert_fusion.6) | copy-start | bytes 786436
  150.1 2.0 %copy-start.4 = (f32[32,7,7]{1,2,0:T(8,128)S(1)}, f32[32,7,7]{1,2,0:T(8,128)}, u32[]{:S(2)}) copy-start(f32[32,7,7]{1,2,0:T(8,128)} %copy.54) | copy-start | bytes 18820
  156.2 4.0 %copy-start.2 = (bf16[64,2048]{1,0:T(8,128)(2,1)S(1)}, bf16[64,2048]{1,0:T(8,128)(2,1)}, u32[]{:S(2)}) copy-start(bf16[64,2048]{1,0:T(8,128)(2,1)} %copy-done.1) | copy-start | bytes 786436
  160.3 1.2 copy-start.5
where the time goes:
time: 163 us; the launch traced here: 162 us
  local copies, waits for them, and re-layouts  45.6 us (28%)
  blocking collectives  41.2 us (25%)
  waiting for transfers between devices  35.2 us (22%)
  matrix products  17.2 us (11%)
  between operations  13.9 us (9%)
  starting transfers between devices  5.33 us (3%)
  other arithmetic  3.17 us (2%)
    psum x1, blocking collectives, shards(): summed = lax.psum((late_sums[0], late_sums[1]), ('ta', 'ga'))  41.2 us
    all_to_all x1, waiting for transfers between devices, shards(): lax.all_to_all(shaped, 'ta', split_axis=1, concat_axis=0, tiled=True)  35.2 us
    another operation x9, local copies, waits for them, and re-layouts, transform(): return jnp.stack(blocks).astype(jnp.bfloat16)  18.4 us
    unnamed x24, local copies, waits for them, and re-layouts  12.7 us
    dot_general x7, matrix products, transform(): jnp.dot(kernel_rows, segment, preferred_element_type=jnp.float32)  8.01 us
    all_to_all x1, local copies, waits for them, and re-layouts, shards(): lax.all_to_all(shaped, 'ta', split_axis=1, concat_axis=0, tiled=True)  6.54 us
    all_to_all x1, starting transfers between devices, shards(): lax.all_to_all(shaped, 'ta', split_axis=1, concat_axis=0, tiled=True)  5.33 us
  transfers between devices with their start and end apart: 1, of which 1 were waited for; matrix products, arithmetic and copies ran while one was open for 1% of the time, Pallas kernels for 0%

commit v1 on v0

--- a/solution.py
+++ b/solution.py
@@ -62,7 +62,10 @@
     own_pts = snapshots.shape[2] // ta_count
     kernel_rows = kernel_table(kept_freqs, jnp.arange(NFFT, dtype=jnp.int32)).astype(jnp.bfloat16)
     shaped = snapshots.reshape(local_times, ta_count, own_pts)
-    arrived = lax.all_to_all(shaped, "ta", split_axis=1, concat_axis=0, tiled=True)
+    size = lax.axis_size("ta")
+    pieces = jnp.stack(jnp.split(shaped, size, axis=1), axis=0)
+    pieces = lax.all_to_all(pieces, "ta", split_axis=0, concat_axis=0)
+    arrived = jnp.concatenate(pieces, axis=0)
     spectra = transform(
         arrived.reshape(arrived.shape[0], arrived.shape[2]), kernel_rows, block_starts
     )

time: 163 us -> 177 us (1.086)
  local copies, waits for them, and re-layouts: 45.6 us -> 57 us
    unnamed x24 -> x35, local copies, waits for them, and re-layouts: 12.7 us -> 22.6 us
    dot_general x7, matrix products: 8.01 us -> 5.47 us  [transform(): jnp.dot(kernel_rows, segment, preferred_element_type=jnp.float32)]
where the time goes in v1:
time: 177 us; the launch traced here: 175 us
  local copies, waits for them, and re-layouts  57 us (32%)
  blocking collectives  41.5 us (23%)
  waiting for transfers between devices  35.4 us (20%)
  matrix products  17.9 us (10%)
  between operations  13.7 us (8%)
  starting transfers between devices  5.33 us (3%)
  other arithmetic  4.52 us (3%)
    psum x1, blocking collectives, shards(): summed = lax.psum((late_sums[0], late_sums[1]), ('ta', 'ga'))  41.5 us
    all_to_all x1, waiting for transfers between devices, shards(): pieces = lax.all_to_all(pieces, 'ta', split_axis=0, concat_axis=0)  35.4 us
    unnamed x35, local copies, waits for them, and re-layouts  22.6 us
    another operation x9, local copies, waits for them, and re-layouts, transform(): return jnp.stack(blocks).astype(jnp.bfloat16)  18.4 us
    all_to_all x1, local copies, waits for them, and re-layouts, shards(): pieces = lax.all_to_all(pieces, 'ta', split_axis=0, concat_axis=0)  6.54 us
    dot_general x7, matrix products, transform(): jnp.dot(kernel_rows, segment, preferred_element_type=jnp.float32)  5.47 us
    all_to_all x1, starting transfers between devices, shards(): pieces = lax.all_to_all(pieces, 'ta', split_axis=0, concat_axis=0)  5.33 us
  transfers between devices with their start and end apart: 1, of which 1 were waited for; matrix products, arithmetic and copies ran while one was open for 1% of the time, Pallas kernels for 0%

profile of v1, /device:TPU:0, one launch (start us, length us, event | category | flops | bytes accessed | tf_op | source)
XLA Modules:
  0.0 175.4 jit_solution(6063164927277509246)
XLA Ops:
  0.6 6.4 %copy.67 = bf16[128,1,16384]{0,2,1:T(8,128)(2,1)} copy(bf16[128,1,16384]{2,0,1:T(8,128)(2,1)} %param.3) | data formatting | bytes 8388608 | tf_op args[0]
  7.0 2.0 %fusion.22 = bf16[8,128,1,2048]{1,3,2,0:T(8,128)(2,1)} fusion(bf16[128,8,2048]{0,2,1:T(8,128)(2,1)} %bitcast.90), kind=kLoop, calls=%fused_computation.42 | loop fusion | bytes 1048576
  9.0 1.9 %fusion.21 = bf16[8,128,1,2048]{1,3,2,0:T(8,128)(2,1)} fusion(bf16[8,128,1,2048]{1,3,2,0:T(8,128)(2,1)} %fusion.22, bf16[128,8,2048]{0,2,1:T(8,128)(2,1)} %bitcast.91), kind=kLoop, calls=%fused_computation.40 | loop fusion | bytes 1048576
  10.9 1.9 %fusion.20 = bf16[8,128,1,2048]{1,3,2,0:T(8,128)(2,1)} fusion(bf16[8,128,1,2048]{1,3,2,0:T(8,128)(2,1)} %fusion.21, bf16[128,8,2048]{0,2,1:T(8,128)(2,1)} %bitcast.92), kind=kLoop, calls=%fused_computation.38 | loop fusion | bytes 1048576
  12.8 1.9 %fusion.19 = bf16[8,128,1,2048]{1,3,2,0:T(8,128)(2,1)} fusion(bf16[8,128,1,2048]{1,3,2,0:T(8,128)(2,1)} %fusion.20, bf16[128,8,2048]{0,2,1:T(8,128)(2,1)} %bitcast.93), kind=kLoop, calls=%fused_computation.36 | loop fusion | bytes 1048576
  14.7 0.8 fusion.18
  15.5 0.8 fusion.17
  16.3 0.8 fusion.16
  17.2 0.9 fusion.15
  18.0 5.3 %all-to-all-start = ((bf16[8,128,1,2048]{1,3,2,0:T(8,128)(2,1)}), bf16[8,128,1,2048]{1,3,2,0:T(8,128)(2,1)}, u32[]{:S(2)}, u32[]{:S(2)}) async-start(bf16[8,128,1,2048]{1,3,2,0:T(8,128)(2,1)} %fusion.15), calls=%async_computation | async-start | bytes 8388608 | tf_op jit(solution)/shard_map/all_to_all | solution.py:67
  23.4 0.7 fusion.37
  37.1 35.4 %all-to-all-done = bf16[8,128,1,2048]{1,3,2,0:T(8,128)(2,1)} async-done(((bf16[8,128,1,2048]{1,3,2,0:T(8,128)(2,1)}), bf16[8,128,1,2048]{1,3,2,0:T(8,128)(2,1)}, u32[]{:S(2)}, u32[]{:S(2)}) %all-to-all-start) | async-done | bytes 4194336 | tf_op jit(solution)/shard_map/all_to_all | solution.py:67
  72.5 6.5 %copy.70 = bf16[8,128,1,2048]{3,1,0,2:T(8,128)(2,1)} copy(bf16[8,128,1,2048]{1,3,2,0:T(8,128)(2,1)} %all-to-all-done) | data formatting | bytes 8388608 | tf_op jit(solution)/shard_map/all_to_all | solution.py:67
  79.1 1.8 %convolution_convert_fusion.5 = bf16[64,2048]{1,0:T(8,128)(2,1)S(1)} fusion(bf16[1024,2048]{1,0:T(8,128)(2,1)} %bitcast.83, s32[]{:T(128)S(6)} %select_n.30, bf16[32,256]{1,0:T(8,128)(2,1)S(1)} %get-tuple-element.22, bf16[32,256]{1,0:T(8,128)(2,1)S(1)} %get-tuple-element.21), kind=kOutput, calls=%fused_computation.10 | convolution fusion | flops 67305472 | bytes 1343492 | tf_op jit(solution)/shard_map/dot_general | solution.py:26
  80.9 1.2 copy.72
  82.1 1.6 convolution_convert_fusion.4
  83.7 1.2 copy.73
  84.9 0.4 convolution_convert_fusion.3
  85.3 1.2 copy.74
  87.0 1.2 copy.75
  88.6 1.2 copy.76
  89.8 0.4 convolution_convert_fusion
  90.2 1.2 copy.77
  91.9 0.7 copy-done.5
  92.6 1.2 copy.71
  93.8 9.9 %stack.100 = bf16[7,2,32,2048]{3,0,2,1:T(8,128)(2,1)S(1)} concatenate(bf16[1,2,32,2048]{3,0,2,1:T(2,128)(2,1)} %copy.71, bf16[1,2,32,2048]{3,0,2,1:T(2,128)(2,1)} %copy.72, bf16[1,2,32,2048]{3,0,2,1:T(2,128)(2,1)} %copy.73, bf16[1,2,32,2048]{3,0,2,1:T(2,128)(2,1)} %copy.74, bf16[1,2,32,2048]{3,0,2,1:T(2,128)(2,1)} %copy.75, bf16[1,2,32,2048]{3,0,2,1:T(2,128)(2,1)} %copy.76, ...), dimensions={0} | concatenate | bytes 3670016 | tf_op jit(solution)/shard_map/stack | solution.py:27
  103.7 1.4 fusion.13
  105.1 1.4 fusion.14
  106.6 1.4 fusion.11
  108.0 0.8 fusion.10
  108.7 1.6 copy.78
  110.4 1.6 copy.79
  112.0 1.6 copy.81
  113.6 0.7 copy.82
  114.3 0.8 add.48
  115.1 0.8 sub.22
  115.9 41.5 %all-reduce = (f32[32,7,7]{0,2,1:T(8,128)}, f32[32,7,7]{0,2,1:T(8,128)S(1)}) all-reduce(f32[32,7,7]{0,2,1:T(8,128)S(1)} %sub.22, f32[32,7,7]{0,2,1:T(8,128)S(1)} %add.48), channel_id=1, replica_groups=mesh['ta'=8,'ga'=4] {'ta','ga'}, use_global_device_ids=true, to_apply=%region_1.2 | all-reduce | flops 3136 | bytes 25088 | tf_op jit(solution)/shard_map/psum | solution.py:73
  157.3 0.6 broadcast_multiply_fusion.1
  158.0 0.9 copy.80
  158.8 2.3 %fusion.12 = f32[32,7,2048]{2,1,0:T(8,128)} fusion(f32[32,7,7]{1,2,0:T(8,128)S(1)} %copy.80, bf16[7,2,32,2048]{3,0,2,1:T(8,128)(2,1)S(1)} %stack.100), kind=kOutput, calls=%fused_computation.24 | convolution fusion | flops 38535168 | bytes 3014656 | tf_op jit(solution)/shard_map/cfp,fcb->bfp/dot_general | solution.py:49
  161.1 1.4 broadcast_multiply_fusion
  162.5 1.5 copy.83
  164.0 2.0 %fusion.9 = f32[32,7,2048]{2,1,0:T(8,128)S(1)} fusion(f32[32,7,7]{1,2,0:T(8,128)} %copy.83, bf16[7,2,32,2048]{3,0,2,1:T(8,128)(2,1)S(1)} %stack.100), kind=kOutput, calls=%fused_computation.21 | convolution fusion | flops 38535168 | bytes 2889856 | tf_op jit(solution)/shard_map/cfp,fcb->bfp/dot_general | solution.py:52
  166.1 2.0 %fusion.1 = f32[7,1,32,2048]{3,0,2,1:T(8,128)S(1)} fusion(f32[32,7,2048]{2,1,0:T(8,128)S(1)} %copy-done.2, f32[32,7,7]{1,2,0:T(8,128)} %copy.83, bf16[7,2,32,2048]{3,0,2,1:T(8,128)(2,1)S(1)} %stack.100), kind=kOutput, calls=%fused_computation.4 | convolution fusion | flops 38993920 | bytes 4987008 | tf_op jit(solution)/shard_map/cfp,fcb->bfp/dot_general | solution.py:49
  168.1 1.1 fusion
  169.2 0.7 maximum_bitcast_fusion
  170.0 4.0 %copy.86 = f32[1,7,2,32,2048]{4,3,2,1,0:T(8,128)} copy(f32[1,7,2,32,2048]{4,1,3,2,0:T(8,128)S(1)} %maximum_bitcast_fusion) | data formatting | bytes 7340032
  174.2 1.2 copy-done.7
  (30 shorter events, 1.7 us)
Async XLA Ops:
  7.0 7.7 %copy-start.1 = (bf16[128,1,16384]{0,2,1:T(8,128)(2,1)S(1)}, bf16[128,1,16384]{0,2,1:T(8,128)(2,1)}, u32[]{:S(2)}) copy-start(bf16[128,1,16384]{0,2,1:T(8,128)(2,1)} %copy.67) | copy-start | bytes 12582916
  18.0 5.3 %copy-start.8 = (s32[7]{0:T(128)S(1)}, s32[7]{0:T(128)}, u32[]{:S(2)}) copy-start(s32[7]{0:T(128)} %param.4) | copy-start | bytes 88
  18.0 18.9 %copy-start.9 = (s32[32]{0:T(128)S(1)}, s32[32]{0:T(128)}, u32[]{:S(2)}) copy-start(s32[32]{0:T(128)} %param.5) | copy-start | bytes 388
  18.0 54.5 %all-to-all-start = ((bf16[8,128,1,2048]{1,3,2,0:T(8,128)(2,1)}), bf16[8,128,1,2048]{1,3,2,0:T(8,128)(2,1)}, u32[]{:S(2)}, u32[]{:S(2)}) async-start(bf16[8,128,1,2048]{1,3,2,0:T(8,128)(2,1)} %fusion.15), calls=%async_computation | async-start | bytes 8388608 | tf_op jit(solution)/shard_map/all_to_all | solution.py:67
  79.1 5.9 %copy-start = (bf16[8,128,1,2048]{3,1,0,2:T(8,128)(2,1)S(1)}, bf16[8,128,1,2048]{3,1,0,2:T(8,128)(2,1)}, u32[]{:S(2)}) copy-start(bf16[8,128,1,2048]{3,1,0,2:T(8,128)(2,1)} %copy.70) | copy-start | bytes 12582916
  90.2 1.6 copy-start.3
  91.9 0.7 copy-start.5
  164.0 2.0 %copy-start.2 = (f32[32,7,2048]{2,1,0:T(8,128)S(1)}, f32[32,7,2048]{2,1,0:T(8,128)}, u32[]{:S(2)}) copy-start(f32[32,7,2048]{2,1,0:T(8,128)} %fusion.12) | copy-start | bytes 5505028
  170.0 4.0 %copy-start.6 = (bf16[64,2048]{1,0:T(8,128)(2,1)S(1)}, bf16[64,2048]{1,0:T(8,128)(2,1)}, u32[]{:S(2)}) copy-start(bf16[64,2048]{1,0:T(8,128)(2,1)} %copy-done.5) | copy-start | bytes 786436
  170.0 4.1 %copy-start.4 = (bf16[64,2048]{1,0:T(8,128)(2,1)S(1)}, bf16[64,2048]{1,0:T(8,128)(2,1)}, u32[]{:S(2)}) copy-start(bf16[64,2048]{1,0:T(8,128)(2,1)} %copy-done.3) | copy-start | bytes 786436
  174.2 1.2 copy-start.7
